TPU v7x, 32 devices: a whole 2x2x4 slice. The times are simulated.
32 devices in a mesh: lat: 16 (over z, y, x), head: 2 (over core).
Axes of the slice: x: 2, y: 2, z: 4, core: 2. Of those that a mesh axis runs over, the one named last changes fastest.
Arguments:
- grid_latent: bfloat16 [131072, 512], P('lat'), may hold values from -6 to 6
- mesh_latent: bfloat16 [10240, 512], P('lat'), may hold values from -6 to 6
- neighbours: int32 [10240, 16], P('lat'), may hold values from -1 to 131071, as said below
- edge_bias: bfloat16 [10240, 64], P('lat', 'head'), may hold values from -8 to 384
- query_weight: bfloat16 [512, 512], P(None, 'head'), may hold values from -0.25 to 0.25
- key_weight: bfloat16 [512, 512], P(None, 'head'), may hold values from -0.25 to 0.25
- value_weight: bfloat16 [512, 512], P(None, 'head'), may hold values from -0.25 to 0.25
- out_weight: bfloat16 [512, 512], P('head'), may hold values from -0.25 to 0.25
- norm_gain: bfloat16 [512], P('head'), may hold values from 0.5 to 1.5
Outputs:
- mesh_out: bfloat16 [10240, 512], P('lat', 'head')
Inputs may be any that keep to these rules, and one draw needn't show every extreme that they name: `neighbours`: every neighbour of mesh node m is -1 or lies in [b * 8192 - 2048, (b + 1) * 8192 + 2048) with b = m // 640; both ends of that range (cut to the grid) are named in every draw; slots 0 and 1 are never -1.
All inputs are finite; a program needn't handle non-finite values.
Results may differ from a plain program's by a relative error of at most 0.0075.
Values may be sent and summed in bfloat16 or wider, within the bound.
A program may use at most 128 MiB of HBM per device.

v0:
```python
import jax
import jax.numpy as jnp
from jax import lax
from jax.sharding import PartitionSpec as P

D = 512
K = 16
HEAD_DIM = 128
HALO = 2048


EPSILON = 1e-05


def extended(block, sides, width):
    for axis, dim in sides:
        count = lax.axis_size(axis)
        forward = [(i, i + 1) for i in range(count - 1)]
        backward = [(target, source) for source, target in forward]
        low = lax.ppermute(
            lax.slice_in_dim(block, block.shape[dim] - width, None, axis=dim), axis, forward
        )
        high = lax.ppermute(lax.slice_in_dim(block, 0, width, axis=dim), axis, backward)
        block = jnp.concatenate([low, block, high], axis=dim)
    return block


def partial_softmax(queries, bias_rows, valid, local, keys, values, local_heads):
    count = queries.shape[0]
    safe_rows = jnp.where(valid, local, 0).reshape(-1)
    key_rows = (
        jnp.take(keys, safe_rows, axis=0)
        .reshape(count, K, local_heads, HEAD_DIM)
        .astype(jnp.float32)
    )
    value_rows = (
        jnp.take(values, safe_rows, axis=0)
        .reshape(count, K, local_heads, HEAD_DIM)
        .astype(jnp.float32)
    )
    query_heads = queries.astype(jnp.float32).reshape(count, local_heads, HEAD_DIM)
    scores = jnp.einsum("nhc,nkhc->nhk", query_heads, key_rows) * HEAD_DIM ** (-0.5)
    scores = scores + bias_rows.astype(jnp.float32).reshape(count, local_heads, K)
    live = valid[:, None, :]
    scores = jnp.where(live, scores, -1e30)
    top_score = jnp.max(scores, axis=2)
    weights = jnp.where(live, jnp.exp(scores - top_score[:, :, None]), 0.0)
    total = jnp.sum(weights, axis=2)
    summed = jnp.einsum("nhk,nkhc->nhc", weights, value_rows)
    return (top_score, total, summed)


def shards(
    grid_latent,
    mesh_latent,
    neighbours,
    edge_bias,
    query_weight,
    key_weight,
    value_weight,
    out_weight,
    norm_gain,
):
    band = grid_latent.shape[0]
    count = mesh_latent.shape[0]
    local_width = key_weight.shape[1]
    local_heads = local_width // HEAD_DIM
    lat_pos = lax.axis_index("lat")
    keys = jnp.dot(grid_latent, key_weight, preferred_element_type=jnp.float32).astype(jnp.bfloat16)
    values = jnp.dot(grid_latent, value_weight, preferred_element_type=jnp.float32).astype(
        jnp.bfloat16
    )
    queries = jnp.dot(mesh_latent, query_weight, preferred_element_type=jnp.float32).astype(
        jnp.bfloat16
    )
    wide_keys, wide_values = (
        extended(keys, (("lat", 0),), HALO),
        extended(values, (("lat", 0),), HALO),
    )
    offset = lat_pos * band - HALO
    valid = neighbours >= 0
    local = jnp.where(valid, neighbours - offset, -1)
    top_score, total, summed = partial_softmax(
        queries, edge_bias, valid, local, wide_keys, wide_values, local_heads
    )
    mixed = summed / total[:, :, None]
    attended = mixed.reshape(count, local_width).astype(jnp.bfloat16)
    projected = jnp.dot(attended, out_weight, preferred_element_type=jnp.float32)
    start = lax.axis_index("head") * local_width
    own_part = lax.psum_scatter(
        projected.astype(jnp.bfloat16), "head", scatter_dimension=1, tiled=True
    ).astype(jnp.float32)
    updated = (
        lax.dynamic_slice_in_dim(mesh_latent, start, local_width, 1).astype(jnp.float32) + own_part
    )
    row_sums, row_squares = lax.psum(
        (jnp.sum(updated, axis=1), jnp.sum(updated * updated, axis=1)), "head"
    )
    mean = row_sums / D
    variance = row_squares / D - mean * mean
    normed = (
        (updated - mean[:, None])
        * lax.rsqrt(variance[:, None] + EPSILON)
        * norm_gain.astype(jnp.float32)
    )
    return normed.astype(jnp.bfloat16)


def solution(mesh):
    in_specs = (
        P("lat", None),
        P("lat", None),
        P("lat", None),
        P("lat", "head"),
        P(None, "head"),
        P(None, "head"),
        P(None, "head"),
        P("head", None),
        P("head"),
    )
    out_specs = P("lat", "head")
    return jax.shard_map(shards, mesh=mesh, in_specs=in_specs, out_specs=out_specs, check_vma=False)
```

profile of v0, /device:TPU:0, one launch (start us, length us, event | category | flops | bytes accessed | tf_op | source)
XLA Modules:
  0.0 268.2 jit_solution(4925674630792918216)
XLA Ops:
  6.5 0.0 reduce-scatter.2.cloned.1.call-start
  6.5 0.9 copy-done
  7.5 5.9 %convolution_convert_fusion.1 = bf16[8192,256]{1,0:T(8,128)(2,1)S(1)} fusion(bf16[8192,512]{1,0:T(8,128)(2,1)} %param.11, bf16[512,256]{1,0:T(8,128)(2,1)S(1)} %copy-done), kind=kOutput, calls=%fused_computation.5 | convolution fusion | flops 2149580800 | bytes 12845056 | tf_op jit(solution)/shard_map/dot_general | solution.py:69
  13.4 0.0 copy-start.3
  13.4 1.6 fusion.19
  15.0 5.9 %collective-permute-start = (bf16[2048,256]{1,0:T(8,128)(2,1)}, bf16[2048,256]{1,0:T(8,128)(2,1)}, u32[]{:S(2)}, u32[]{:S(2)}) collective-permute-start(bf16[2048,256]{1,0:T(8,128)(2,1)} %get-tuple-element.12), channel_id=1, source_target_pairs={{0,2},{2,4},{4,6},{6,8},{8,10},{10,12},{12,14},{14,16},{16,18},{18... | collective-permute-start | bytes 3145736 | tf_op jit(solution)/shard_map/ppermute | solution.py:20
  20.8 0.0 copy-done.3
  20.8 1.4 collective-permute-start.1
  22.3 0.0 copy-done.9
  22.3 0.0 copy-done.8
  22.3 2.3 convolution_convert_fusion
  24.6 0.0 copy-start.2
  24.6 2.0 copy-done.2
  26.7 1.5 fusion.18
  28.1 4.6 %collective-permute-start.2 = (bf16[2048,256]{1,0:T(8,128)(2,1)}, bf16[2048,256]{1,0:T(8,128)(2,1)S(1)}, u32[]{:S(2)}, u32[]{:S(2)}) collective-permute-start(bf16[2048,256]{1,0:T(8,128)(2,1)} %get-tuple-element.10), channel_id=1, source_target_pairs={{0,2},{2,4},{4,6},{6,8},{8,10},{10,12},{12,14},{14,16},{16,18},{18... | collective-permute-start | bytes 3145736 | tf_op jit(solution)/shard_map/ppermute | solution.py:20
  32.7 1.3 collective-permute-start.3
  34.1 0.2 copy.11
  34.2 0.1 reshape.34
  34.4 0.0 copy-done.4
  34.4 0.0 copy-done.5
  34.4 0.4 convolution_convert_fusion.3
  34.8 0.9 copy.23
  35.8 52.8 %collective-permute-done = bf16[2048,256]{1,0:T(8,128)(2,1)} collective-permute-done((bf16[2048,256]{1,0:T(8,128)(2,1)}, bf16[2048,256]{1,0:T(8,128)(2,1)}, u32[]{:S(2)}, u32[]{:S(2)}) %collective-permute-start) | collective-permute-done | bytes 1048608 | tf_op jit(solution)/shard_map/ppermute | solution.py:20
  88.6 0.0 collective-permute-done.1
  88.6 8.6 %pad_maximum_fusion = bf16[12288,256]{1,0:T(8,128)(2,1)} fusion(bf16[2048,256]{1,0:T(8,128)(2,1)} %collective-permute-done.1, bf16[8192,256]{1,0:T(8,128)(2,1)} %copy-done.3, bf16[2048,256]{1,0:T(8,128)(2,1)} %collective-permute-done), kind=kLoop, calls=%fused_computation.6 | loop fusion | flops 18874368 | bytes 12582912 | tf_op jit(solution)/shard_map/concatenate | solution.py:24
  97.2 42.0 %gather_fusion = bf16[10240,256]{1,0:T(8,128)(2,1)} fusion(bf16[12288,256]{1,0:T(8,128)(2,1)} %pad_maximum_fusion, s32[10240]{0:T(1024)S(1)} %fusion.15), kind=kCustom, calls=%fused_computation.clone | custom fusion | bytes 10526720 | tf_op jit(solution)/shard_map/jit(_take)/gather | solution.py:32
  139.2 0.0 collective-permute-done.2
  139.2 0.0 collective-permute-done.3
  139.2 12.0 %pad_maximum_fusion.1 = bf16[12288,256]{1,0:T(8,128)(2,1)} fusion(bf16[2048,256]{1,0:T(8,128)(2,1)} %collective-permute-done.3, bf16[8192,256]{1,0:T(8,128)(2,1)} %copy-done.2, bf16[2048,256]{1,0:T(8,128)(2,1)S(1)} %collective-permute-done.2), kind=kLoop, calls=%fused_computation.7 | loop fusion | flops 18874368 | bytes 12582912 | tf_op jit(solution)/shard_map/concatenate | solution.py:24
  151.2 42.0 %gather_fusion.1 = bf16[10240,256]{1,0:T(8,128)(2,1)} fusion(bf16[12288,256]{1,0:T(8,128)(2,1)} %pad_maximum_fusion.1, s32[10240]{0:T(1024)S(1)} %fusion.15), kind=kCustom, calls=%fused_computation.1.clone | custom fusion | bytes 10526720 | tf_op jit(solution)/shard_map/jit(_take)/gather | solution.py:37
  193.2 10.6 %broadcast_select_fusion = (bf16[10240,256]{1,0:T(8,128)(2,1)}, bf16[10240,256]{1,0:T(8,128)(2,1)}) fusion(bf16[10240,256]{1,0:T(8,128)(2,1)} %gather_fusion.1, pred[10240]{0:T(1024)(128)(4,1)S(1)} %compare_and_fusion, bf16[10240,256]{1,0:T(8,128)(2,1)} %gather_fusion), kind=kLoop, calls=%fused_computation.10 | loop fusion | flops 5242880 | bytes 20981760 | tf_op jit(solution)/shard_map/jit(_take)/select_n | solution.py:37
  203.7 8.3 %reshape.35 = bf16[640,16,2,128]{3,2,1,0:T(2,128)(2,1)} reshape(bf16[10240,256]{1,0:T(8,128)(2,1)} %get-tuple-element.15) | data formatting | bytes 10485760 | tf_op jit(solution)/shard_map/reshape | solution.py:33
  212.0 15.3 %multiply_reduce_fusion = f32[640,2,16]{1,2,0:T(8,128)} fusion(f32[640,2,128]{2,1,0:T(2,128)S(1)} %copy.23, bf16[640,16,2,128]{3,2,1,0:T(2,128)(2,1)} %reshape.35), kind=kLoop, calls=%fused_computation.3 | loop fusion | flops 7843840 | bytes 5980160
  227.3 3.3 %copy.19 = f32[640,2,16]{0,2,1:T(8,128)S(1)} copy(f32[640,2,16]{1,2,0:T(8,128)} %multiply_reduce_fusion) | data formatting | bytes 163840 | tf_op jit(solution)/shard_map/nhc,nkhc->nhk/dot_general | solution.py:42
  230.6 0.0 copy-done.10
  230.6 0.1 fusion.20
  230.7 0.9 copy.20
  231.5 8.5 %reshape.38 = bf16[640,16,2,128]{3,2,1,0:T(2,128)(2,1)} reshape(bf16[10240,256]{1,0:T(8,128)(2,1)} %get-tuple-element.14) | data formatting | bytes 10485760 | tf_op jit(solution)/shard_map/reshape | solution.py:38
  240.1 0.2 copy.12
  240.3 4.0 %fusion.1 = f32[640,2,1,128]{3,2,1,0:T(1,128)S(1)} fusion(bf16[640,2,16,1]{2,3,1,0:T(2,128)(2,1)S(1)} %copy.20, bf16[640,16,2,128]{3,2,1,0:T(2,128)(2,1)} %reshape.38), kind=kOutput, calls=%fused_computation.8 | convolution fusion | flops 5242880 | bytes 5939200 | tf_op jit(solution)/shard_map/nhk,nkhc->nhc/dot_general | solution.py:49
  244.3 0.9 divide_convert_fusion
  245.1 0.0 copy-done.6
  245.1 1.2 convolution_convert_fusion.2
  246.3 0.0 reduce-scatter.2.cloned.1.call-update
  246.4 9.3 %reduce-scatter.2.cloned.1.call-done = bf16[640,256]{1,0:T(8,128)(2,1)} async-done(((bf16[640,512]{1,0:T(8,128)(2,1)}), bf16[640,256]{1,0:T(8,128)(2,1)}) %reduce-scatter.2.cloned.1.call-update) | async-done | bytes 327696 | tf_op jit(solution)/shard_map/reduce_scatter | solution.py:90
  255.6 1.2 fusion.6
  256.9 2.5 all-reduce
  259.4 1.9 multiply_convert_fusion
  (19 shorter events, 0.1 us)
Async XLA Ops:
  6.5 1.0 copy-start
  6.5 15.7 %copy-start.9 = (bf16[512,256]{1,0:T(8,128)(2,1)S(1)}, bf16[512,256]{1,0:T(8,128)(2,1)}, u32[]{:S(2)}) copy-start(bf16[512,256]{1,0:T(8,128)(2,1)} %param.17) | copy-start | bytes 786436
  6.5 249.1 %reduce-scatter.2.cloned.1.call-start = ((), (), s32[]{:S(2)}) async-start(), calls=%async_computation.1 | async-start | bytes 983040 | tf_op jit(solution)/shard_map/reduce_scatter | solution.py:90
  7.5 14.8 %copy-start.8 = (bf16[8192,512]{1,0:T(8,128)(2,1)S(1)}, bf16[8192,512]{1,0:T(8,128)(2,1)}, u32[]{:S(2)}) copy-start(bf16[8192,512]{1,0:T(8,128)(2,1)} %param.11) | copy-start | bytes 25165828
  13.4 7.4 %copy-start.3 = (bf16[8192,256]{1,0:T(8,128)(2,1)}, bf16[8192,256]{1,0:T(8,128)(2,1)S(1)}, u32[]{:S(2)}) copy-start(bf16[8192,256]{1,0:T(8,128)(2,1)S(1)} %convolution_convert_fusion.1) | copy-start | bytes 12582916
  15.0 73.7 %collective-permute-start = (bf16[2048,256]{1,0:T(8,128)(2,1)}, bf16[2048,256]{1,0:T(8,128)(2,1)}, u32[]{:S(2)}, u32[]{:S(2)}) collective-permute-start(bf16[2048,256]{1,0:T(8,128)(2,1)} %get-tuple-element.12), channel_id=1, source_target_pairs={{0,2},{2,4},{4,6},{6,8},{8,10},{10,12},{12,14},{14,16},{16,18},{18... | collective-permute-start | bytes 3145736 | tf_op jit(solution)/shard_map/ppermute | solution.py:20
  20.8 13.2 %copy-start.7 = (s32[640,16]{0,1:T(8,128)S(1)}, s32[640,16]{0,1:T(8,128)}, u32[]{:S(2)}) copy-start(s32[640,16]{0,1:T(8,128)} %param.13) | copy-start | bytes 122884
  20.8 13.6 %copy-start.4 = (bf16[640,512]{1,0:T(8,128)(2,1)S(1)}, bf16[640,512]{1,0:T(8,128)(2,1)}, u32[]{:S(2)}) copy-start(bf16[640,512]{1,0:T(8,128)(2,1)} %param.12) | copy-start | bytes 1966084
  20.8 13.6 %copy-start.5 = (bf16[512,256]{1,0:T(8,128)(2,1)S(1)}, bf16[512,256]{1,0:T(8,128)(2,1)}, u32[]{:S(2)}) copy-start(bf16[512,256]{1,0:T(8,128)(2,1)} %param.15) | copy-start | bytes 786436
  20.8 67.8 %collective-permute-start.1 = (bf16[2048,256]{1,0:T(8,128)(2,1)}, bf16[2048,256]{1,0:T(8,128)(2,1)}, u32[]{:S(2)}, u32[]{:S(2)}) collective-permute-start(bf16[2048,256]{1,0:T(8,128)(2,1)} %get-tuple-element.13), channel_id=1, source_target_pairs={{2,0},{4,2},{6,4},{8,6},{10,8},{12,10},{14,12},{16,14},{18,16},{20... | collective-permute-start | bytes 3145736 | tf_op jit(solution)/shard_map/ppermute | solution.py:23
  24.6 2.0 copy-start.2
  28.1 111.1 %collective-permute-start.2 = (bf16[2048,256]{1,0:T(8,128)(2,1)}, bf16[2048,256]{1,0:T(8,128)(2,1)S(1)}, u32[]{:S(2)}, u32[]{:S(2)}) collective-permute-start(bf16[2048,256]{1,0:T(8,128)(2,1)} %get-tuple-element.10), channel_id=1, source_target_pairs={{0,2},{2,4},{4,6},{6,8},{8,10},{10,12},{12,14},{14,16},{16,18},{18... | collective-permute-start | bytes 3145736 | tf_op jit(solution)/shard_map/ppermute | solution.py:20
  32.7 106.5 %collective-permute-start.3 = (bf16[2048,256]{1,0:T(8,128)(2,1)}, bf16[2048,256]{1,0:T(8,128)(2,1)}, u32[]{:S(2)}, u32[]{:S(2)}) collective-permute-start(bf16[2048,256]{1,0:T(8,128)(2,1)} %get-tuple-element.11), channel_id=1, source_target_pairs={{2,0},{4,2},{6,4},{8,6},{10,8},{12,10},{14,12},{16,14},{18,16},{20... | collective-permute-start | bytes 3145736 | tf_op jit(solution)/shard_map/ppermute | solution.py:23
  212.0 18.6 %copy-start.10 = (bf16[640,32]{0,1:T(8,128)(2,1)S(1)}, bf16[640,32]{0,1:T(8,128)(2,1)}, u32[]{:S(2)}) copy-start(bf16[640,32]{0,1:T(8,128)(2,1)} %param.14) | copy-start | bytes 122884
  240.1 5.0 %copy-start.6 = (bf16[256,512]{1,0:T(8,128)(2,1)S(1)}, bf16[256,512]{1,0:T(8,128)(2,1)}, u32[]{:S(2)}) copy-start(bf16[256,512]{1,0:T(8,128)(2,1)} %param.18) | copy-start | bytes 786436
  240.1 6.3 %copy-start.11 = (bf16[256]{0:T(256)(128)(2,1)S(1)}, bf16[256]{0:T(256)(128)(2,1)}, u32[]{:S(2)}) copy-start(bf16[256]{0:T(256)(128)(2,1)} %param.19) | copy-start | bytes 1540
  240.1 21.2 %copy-start.1 = (bf16[512,256]{1,0:T(8,128)(2,1)S(1)}, bf16[512,256]{1,0:T(8,128)(2,1)}, u32[]{:S(2)}) copy-start(bf16[512,256]{1,0:T(8,128)(2,1)} %param.16) | copy-start | bytes 786436
Sparse Core Ops, SparseCore 0:
  246.5 9.1 reduce-scatter.1
where the time goes:
time: 269 us; the launch traced here: 268 us
  local copies, waits for them, and re-layouts  112 us (42%)
  waiting for transfers between devices  62.1 us (23%)
  other arithmetic  50.6 us (19%)
  matrix products  13.8 us (5%)
  between operations  13.6 us (5%)
  starting transfers between devices  13.2 us (5%)
    ppermute x2, waiting for transfers between devices, extended(): lax.ppermute(lax.slice_in_dim(block, block.shape[dim] - width, None, axis...  52.8 us
    gather x1, local copies, waits for them, and re-layouts, partial_softmax(): jnp.take(keys, safe_rows, axis=0).reshape(count, K, local_heads, HEAD_DIM)  42 us
    gather x1, local copies, waits for them, and re-layouts, partial_softmax(): jnp.take(values, safe_rows, axis=0).reshape(count, K, local_heads, HEAD_DIM)  42 us
    concatenate x2, other arithmetic, extended(): block = jnp.concatenate([low, block, high], axis=dim)  20.6 us
    unnamed x1, other arithmetic  15.3 us
    select_n x1, other arithmetic, partial_softmax(): jnp.take(values, safe_rows, axis=0).reshape(count, K, local_heads, HEAD_DIM)  10.6 us
    ppermute x2, starting transfers between devices, extended(): lax.ppermute(lax.slice_in_dim(block, block.shape[dim] - width, None, axis...  10.5 us
    reduce_scatter x1, waiting for transfers between devices, shards(): lax.psum_scatter(projected.astype(jnp.bfloat16), 'head', scatter_dimensio...  9.29 us
  transfers between devices with their start and end apart: 5, of which 2 were waited for; matrix products, arithmetic and copies ran while one was open for 21% of the time, Pallas kernels for 0%

commit v1 on v0

v1 whole, which is shorter than its diff:
```python
import functools

import jax
import jax.numpy as jnp
from jax import lax
from jax.experimental import pallas as pl
from jax.experimental.pallas import tpu as pltpu
from jax.sharding import PartitionSpec as P

K = 16
HEAD_DIM = 128
HALO = 2048
LANES = 128
SUB = 8
NODES = LANES // K
EPSILON = 1e-05
DEAD = -1e30
PIECE = 1024
UNROLL = 4


def attend(
    order_ref,
    grid_ref,
    low_own,
    low_other,
    high_own,
    high_other,
    query_ref,
    bias_ref,
    mesh_ref,
    value_ref,
    out_weight_ref,
    gain_ref,
    out_ref,
    wide,
    picked,
    mixed,
    stage,
    sems,
):
    width = grid_ref.shape[1]
    cols = width // LANES
    band = grid_ref.shape[0]
    edges = picked.shape[0] // cols
    heads = width // HEAD_DIM
    chunk_rows = heads * NODES
    chunks = edges // LANES
    half = low_own.shape[0]
    me = lax.axis_index("head")

    pieces = []
    for start in range(0, band, PIECE):
        pieces.append((grid_ref, start, HALO + start))
    for start in range(0, half, PIECE):
        pieces.append((low_own, start, me * half + start))
        pieces.append((low_other, start, (1 - me) * half + start))
        pieces.append((high_own, start, HALO + band + me * half + start))
        pieces.append((high_other, start, HALO + band + (1 - me) * half + start))

    def fetch(n):
        ref, start, _ = pieces[n]
        return pltpu.make_async_copy(
            ref.at[pl.ds(start, PIECE)], stage.at[n % 2], sems.at[n % 2]
        )

    fetch(0).start()
    for n in range(len(pieces)):
        if n + 1 < len(pieces):
            fetch(n + 1).start()
        fetch(n).wait()
        base = pieces[n][2] * cols

        def widen(step, carry, n=n, base=base):
            for part in range(2):
                row = pl.multiple_of(step * 32 + part * 16, 16)
                block = stage[n % 2, pl.ds(row, 16), :].astype(jnp.float32)
                for t in range(2):
                    for c in range(cols):
                        at = pl.multiple_of(base + row * cols + (t * cols + c) * SUB, SUB)
                        wide[pl.ds(at, SUB), :] = block[
                            t * SUB : (t + 1) * SUB, c * LANES : (c + 1) * LANES
                        ]
            return carry

        lax.fori_loop(0, PIECE // 32, widen, 0)

    def pick(step, carry):
        for e in range(32):
            at = order_ref[step * 32 + e]
            row = wide[pl.ds(at, cols, stride=SUB), :]
            to = step * (32 * cols) + (e // SUB) * (cols * SUB) + e % SUB
            picked[pl.ds(to, cols, stride=SUB), :] = row
        return carry

    lax.fori_loop(0, edges // 32, pick, 0)

    tiles = LANES // SUB

    def score(step, carry):
        for u in range(UNROLL):
            chunk = step * UNROLL + u
            start = chunk * (LANES * cols)
            parts = []
            for c in range(cols):
                parts.append(
                    jnp.concatenate(
                        [
                            picked[
                                pl.ds(
                                    pl.multiple_of(start + (t * cols + c) * SUB, SUB), SUB
                                ),
                                :,
                            ]
                            for t in range(tiles)
                        ],
                        axis=0,
                    ).astype(jnp.bfloat16)
                )
            rows = jnp.concatenate(parts, axis=1)
            at = pl.ds(pl.multiple_of(chunk * chunk_rows, chunk_rows), chunk_rows)
            scores = lax.dot_general(
                query_ref[at, :],
                rows,
                (((1,), (1,)), ((), ())),
                preferred_element_type=jnp.float32,
            )
            scores = scores * HEAD_DIM ** (-0.5) + bias_ref[at, :]
            top = jnp.max(scores, axis=1, keepdims=True)
            weights = jnp.exp(scores - top)
            total = jnp.sum(weights, axis=1, keepdims=True)
            summed = jnp.dot(
                weights.astype(jnp.bfloat16), rows, preferred_element_type=jnp.float32
            )
            summed = summed / total
            for h in range(heads):
                mixed[h, pl.ds(pl.multiple_of(chunk * NODES, NODES), NODES), :] = summed[
                    h * NODES : (h + 1) * NODES
                ]
        return carry

    lax.fori_loop(0, chunks // UNROLL, score, 0)

    attended = jnp.concatenate(
        [
            jnp.dot(
                mixed[h].astype(jnp.bfloat16),
                value_ref[:, h * HEAD_DIM : (h + 1) * HEAD_DIM],
                preferred_element_type=jnp.float32,
            ).astype(jnp.bfloat16)
            for h in range(heads)
        ],
        axis=1,
    )
    updated = mesh_ref[...].astype(jnp.float32) + jnp.dot(
        attended, out_weight_ref[...], preferred_element_type=jnp.float32
    )
    mean = jnp.sum(updated, axis=1, keepdims=True) / width
    variance = jnp.sum(updated * updated, axis=1, keepdims=True) / width - mean * mean
    normed = (updated - mean) * lax.rsqrt(variance + EPSILON) * gain_ref[...]
    out_ref[...] = normed.astype(jnp.bfloat16)


def swap(block):
    return lax.ppermute(block, "head", [(0, 1), (1, 0)])


def ordered(own, other, me, axis):
    first = jnp.where(me == 0, own, other)
    second = jnp.where(me == 0, other, own)
    return jnp.concatenate([first, second], axis=axis)


def shards(
    grid_latent,
    mesh_latent,
    neighbours,
    edge_bias,
    query_weight,
    key_weight,
    value_weight,
    out_weight,
    norm_gain,
):
    band, width = grid_latent.shape
    count = mesh_latent.shape[0]
    part = count // 2
    cols = width // LANES
    heads = width // HEAD_DIM
    edges = part * K
    half = HALO // 2
    me = lax.axis_index("head")
    lat = lax.axis_index("lat")
    size = lax.axis_size("lat")
    forward = [(i, i + 1) for i in range(size - 1)]
    backward = [(i + 1, i) for i in range(size - 1)]
    low_own = lax.ppermute(
        lax.dynamic_slice_in_dim(grid_latent, band - HALO + me * half, half, 0), "lat", forward
    )
    high_own = lax.ppermute(
        lax.dynamic_slice_in_dim(grid_latent, me * half, half, 0), "lat", backward
    )
    low_other = swap(low_own)
    high_other = swap(high_own)

    query_all = ordered(query_weight, swap(query_weight), me, 1)
    key_all = ordered(key_weight, swap(key_weight), me, 1)
    value_all = ordered(value_weight, swap(value_weight), me, 1)
    out_all = ordered(out_weight, swap(out_weight), me, 0)
    gain_all = ordered(norm_gain, swap(norm_gain), me, 0)
    bias_own = lax.dynamic_slice_in_dim(edge_bias, me * part, part, 0)
    bias_other = swap(lax.dynamic_slice_in_dim(edge_bias, (1 - me) * part, part, 0))
    bias_all = ordered(bias_own, bias_other, me, 1)

    mesh_rows = lax.dynamic_slice_in_dim(mesh_latent, me * part, part, 0)
    neigh = lax.dynamic_slice_in_dim(neighbours, me * part, part, 0)
    valid = neigh >= 0
    local = jnp.where(valid, neigh - (lat * band - HALO), HALO)
    order = ((local // SUB) * (SUB * cols) + local % SUB).reshape(-1)

    queries = jnp.dot(mesh_rows, query_all, preferred_element_type=jnp.float32).astype(
        jnp.bfloat16
    )
    folded = jnp.einsum(
        "xnhc,dhc->xhnd",
        queries.reshape(part // NODES, NODES, heads, HEAD_DIM),
        key_all.reshape(width, heads, HEAD_DIM),
        preferred_element_type=jnp.float32,
    ).astype(jnp.bfloat16)
    folded = folded.reshape(part * heads, width)

    spread = (
        jnp.arange(K, dtype=jnp.int32)[:, None]
        == (jnp.arange(LANES, dtype=jnp.int32) % K)[None, :]
    ).astype(jnp.bfloat16)
    bias_rows = bias_all.reshape(part // NODES, NODES, heads, K).transpose(0, 2, 1, 3)
    bias_rows = jnp.dot(
        bias_rows.reshape(part * heads, K), spread, preferred_element_type=jnp.float32
    ).reshape(part // NODES, heads, NODES, LANES)
    live = jnp.dot(valid.astype(jnp.bfloat16), spread, preferred_element_type=jnp.float32)
    live = live.reshape(part // NODES, 1, NODES, LANES) > 0.5
    own_lane = (
        jnp.arange(NODES, dtype=jnp.int32)[:, None]
        == (jnp.arange(LANES, dtype=jnp.int32) // K)[None, :]
    )
    bias_rows = jnp.where(live & own_lane, bias_rows, DEAD).reshape(part * heads, LANES)

    vmem = pl.BlockSpec(memory_space=pltpu.VMEM)
    hbm = pl.BlockSpec(memory_space=pl.ANY)
    normed = pl.pallas_call(
        attend,
        name="attend",
        out_shape=jax.ShapeDtypeStruct((part, width), jnp.bfloat16),
        in_specs=[pl.BlockSpec(memory_space=pltpu.SMEM)] + [hbm] * 5 + [vmem] * 6,
        out_specs=vmem,
        scratch_shapes=[
            pltpu.VMEM(((band + 2 * HALO) * cols, LANES), jnp.float32),
            pltpu.VMEM((edges * cols, LANES), jnp.float32),
            pltpu.VMEM((heads, part, width), jnp.float32),
            pltpu.VMEM((2, PIECE, width), jnp.bfloat16),
            pltpu.SemaphoreType.DMA((2,)),
        ],
        compiler_params=pltpu.CompilerParams(vmem_limit_bytes=58 * 1024 * 1024),
    )(
        order,
        grid_latent,
        low_own,
        low_other,
        high_own,
        high_other,
        folded,
        bias_rows,
        mesh_rows,
        value_all,
        out_all,
        gain_all.astype(jnp.float32).reshape(1, width),
    )
    side = width // 2
    keep = lax.dynamic_slice_in_dim(normed, me * side, side, 1)
    give = swap(lax.dynamic_slice_in_dim(normed, (1 - me) * side, side, 1))
    return ordered(keep, give, me, 0)


def solution(mesh):
    in_specs = (
        P("lat", None),
        P("lat", None),
        P("lat", None),
        P("lat", "head"),
        P(None, "head"),
        P(None, "head"),
        P(None, "head"),
        P("head", None),
        P("head"),
    )
    out_specs = P("lat", "head")
    return jax.shard_map(shards, mesh=mesh, in_specs=in_specs, out_specs=out_specs, check_vma=False)
```

time: 269 us -> 103 us (0.38)
  local copies, waits for them, and re-layouts: 112 us -> 7.58 us
  other arithmetic: 50.6 us -> 8.12 us
  Pallas kernels: 0 us -> 31.9 us
  waiting for transfers between devices: 62.1 us -> 41.4 us
  between operations: 13.6 us -> 0.24 us
  matrix products: 13.8 us -> 3.23 us
  starting transfers between devices: 13.2 us -> 9.6 us
    gather x2 -> x0, local copies, waits for them, and re-layouts: 83.9 us -> none  [the longest x1 42 us: partial_softmax(): jnp.take(keys, safe_rows, axis=0).reshape(count, K, local_heads, HEAD_DIM)]
    pallas_call x0 -> x1, Pallas kernels: none -> 31.9 us  [shards(): pl.pallas_call(attend, name='attend', out_shape=jax.ShapeDtypeStruct((par...]
    concatenate x2 -> x5, other arithmetic: 20.6 us -> 2.46 us  [ordered(): return jnp.concatenate([first, second], axis=axis)]
    reshape x3, local copies, waits for them, and re-layouts: 17 us -> 1.02 us  [the longest x1 0.71 us: shards(): order = (local // SUB * (SUB * cols) + local % SUB).reshape(-1)]
    unnamed x1 -> x0, other arithmetic: 15.3 us -> none
    ppermute x4 -> x11, waiting for transfers between devices: 52.8 us -> 41.4 us  [the longest x1 23.4 us: shards(): lax.ppermute(lax.dynamic_slice_in_dim(grid_latent, band - HALO + me * hal...]
    dot_general x5 -> x4, matrix products: 13.8 us -> 3.23 us  [the longest x1 1.37 us: shards(): jnp.dot(mesh_rows, query_all, preferred_element_type=jnp.float32)]
    reduce_scatter x1 -> x0, waiting for transfers between devices: 9.29 us -> none  [shards(): lax.psum_scatter(projected.astype(jnp.bfloat16), 'head', scatter_dimensio...]
  transfers between devices with their start and end apart: 5 -> 11, of which waited for: 2 -> 3; matrix products, arithmetic and copies ran while one was open for 21% -> 16% of each run, Pallas kernels for 0% -> 0%
where the time goes in v1:
time: 103 us; the launch traced here: 102 us
  waiting for transfers between devices  41.4 us (40%)
  Pallas kernels  31.9 us (31%)
  starting transfers between devices  9.6 us (9%)
  other arithmetic  8.12 us (8%)
  local copies, waits for them, and re-layouts  7.58 us (7%)
  matrix products  3.23 us (3%)
    pallas_call x1, Pallas kernels, shards(): pl.pallas_call(attend, name='attend', out_shape=jax.ShapeDtypeStruct((par...  31.9 us
    ppermute x1, waiting for transfers between devices, shards(): lax.ppermute(lax.dynamic_slice_in_dim(grid_latent, band - HALO + me * hal...  23.4 us
    ppermute x1, waiting for transfers between devices, shards(): lax.ppermute(lax.dynamic_slice_in_dim(grid_latent, me * half, half, 0), '...  17 us
    ppermute x1, starting transfers between devices, shards(): lax.ppermute(lax.dynamic_slice_in_dim(grid_latent, band - HALO + me * hal...  6.09 us
    select_n x6, other arithmetic, ordered(): first = jnp.where(me == 0, own, other)  4.07 us
    dynamic_slice x1, local copies, waits for them, and re-layouts, shards(): lax.dynamic_slice_in_dim(grid_latent, me * half, half, 0)  3.02 us
    concatenate x5, other arithmetic, ordered(): return jnp.concatenate([first, second], axis=axis)  2.46 us
    ppermute x9, starting transfers between devices, swap(): return lax.ppermute(block, 'head', [(0, 1), (1, 0)])  2.23 us
  transfers between devices with their start and end apart: 11, of which 3 were waited for; matrix products, arithmetic and copies ran while one was open for 16% of the time, Pallas kernels for 0%

profile of v1, /device:TPU:0, one launch (start us, length us, event | category | flops | bytes accessed | tf_op | source)
XLA Modules:
  0.0 102.1 jit_solution(264352749190445593)
XLA Ops:
  0.0 0.5 collective-permute-start.9
  0.5 0.8 constant_dynamic-slice_fusion.1
  1.3 0.1 collective-permute-start.6
  1.4 0.4 collective-permute-start.5
  1.8 0.1 collective-permute-start.4
  1.9 0.4 collective-permute-start.7
  2.4 0.0 copy-start.1
  2.4 0.0 copy-start.8
  2.4 0.0 copy-start.7
  2.4 1.0 fusion.12
  3.4 0.2 fusion.3
  3.7 3.0 %constant_dynamic-slice_fusion.3 = (bf16[1024,512]{1,0:T(8,128)(2,1)}, bf16[1024,512]{1,0:T(8,128)(2,1)}) fusion(bf16[8192,512]{1,0:T(8,128)(2,1)} %grid_ref.1, s32[]{:T(128)S(6)} %select_n.143, s32[]{:T(128)S(6)} %select_n.142), kind=kLoop, calls=%fused_computation.55 | loop fusion | bytes 4194312 | tf_op jit(solution)/shard_map/dynamic_slice | solution.py:201
  6.7 0.1 copy.13
  6.8 0.7 reshape.108.order_ref
  7.5 0.0 collective-permute-done.9
  7.5 1.3 %collective-permute-start.2 = (bf16[1024,512]{1,0:T(8,128)(2,1)}, bf16[1024,512]{1,0:T(8,128)(2,1)S(1)}, u32[]{:S(2)}, u32[]{:S(2)}) collective-permute-start(bf16[1024,512]{1,0:T(8,128)(2,1)} %get-tuple-element.7), channel_id=1, source_target_pairs={{2,0},{4,2},{6,4},{8,6},{10,8},{12,10},{14,12},{16,14},{18,16},{20... | collective-permute-start | bytes 3145736 | tf_op jit(solution)/shard_map/ppermute | solution.py:200
  8.9 0.6 maximum_convert_fusion.gain_ref
  9.4 0.0 collective-permute-done.6
  9.4 6.1 %collective-permute-start = (bf16[1024,512]{1,0:T(8,128)(2,1)}, bf16[1024,512]{1,0:T(8,128)(2,1)}, u32[]{:S(2)}, u32[]{:S(2)}) collective-permute-start(bf16[1024,512]{1,0:T(8,128)(2,1)} %get-tuple-element.8), channel_id=1, source_target_pairs={{0,2},{2,4},{4,6},{6,8},{8,10},{10,12},{12,14},{14,16},{16,18},{18... | collective-permute-start | bytes 3145736 | tf_op jit(solution)/shard_map/ppermute | solution.py:197
  15.5 0.1 broadcast_select_fusion.11
  15.6 0.1 copy.17
  15.8 0.2 reshape.112
  15.9 1.1 %convolution_select_fusion = f32[40,4,8,128]{3,2,1,0:T(8,128)} fusion(bf16[40,8,4,16]{3,2,1,0:T(4,128)(2,1)S(1)} %reshape.112, pred[40,8,128]{2,1,0:T(8,128)(4,1)S(1)} %fusion.3, s32[128]{0:T(128)S(1)} %get-tuple-element.24), kind=kOutput, calls=%fused_computation.2 | convolution fusion | flops 5408768 | bytes 737792 | tf_op jit(solution)/shard_map/dot_general | solution.py:237
  17.0 0.0 collective-permute-done.4
  17.0 0.1 collective-permute-start.8
  17.2 1.1 %broadcast_select_fusion.7 = (bf16[512,256]{1,0:T(8,128)(2,1)S(1)}, bf16[512,256]{1,0:T(8,128)(2,1)S(1)}) fusion(bf16[512,256]{1,0:T(8,128)(2,1)} %param.14, bf16[512,256]{1,0:T(8,128)(2,1)} %collective-permute-done.4, pred[]{:T(512)S(6)} %eq.28), kind=kLoop, calls=%fused_computation.26 | loop fusion | flops 262144 | bytes 1048577 | tf_op jit(solution)/shard_map/jit(_where)/select_n | solution.py:169
  18.2 0.0 collective-permute-done.5
  18.2 0.0 collective-permute-done.7
  18.3 0.9 broadcast_select_fusion.3
  19.2 17.0 %collective-permute-done.2.high_own = bf16[1024,512]{1,0:T(8,128)(2,1)S(1)} collective-permute-done((bf16[1024,512]{1,0:T(8,128)(2,1)}, bf16[1024,512]{1,0:T(8,128)(2,1)S(1)}, u32[]{:S(2)}, u32[]{:S(2)}) %collective-permute-start.2) | collective-permute-done | bytes 1048608 | tf_op jit(solution)/shard_map/ppermute | solution.py:200
  36.2 0.0 collective-permute-start.3
  36.2 23.4 %collective-permute-done.low_own = bf16[1024,512]{1,0:T(8,128)(2,1)} collective-permute-done((bf16[1024,512]{1,0:T(8,128)(2,1)}, bf16[1024,512]{1,0:T(8,128)(2,1)}, u32[]{:S(2)}, u32[]{:S(2)}) %collective-permute-start) | collective-permute-done | bytes 1048608 | tf_op jit(solution)/shard_map/ppermute | solution.py:197
  59.6 0.1 collective-permute-start.1
  59.7 0.1 reshape.109
  59.9 1.4 %fusion.1 = bf16[40,8,4,128]{3,1,2,0:T(8,128)(2,1)S(1)} fusion(bf16[320,512]{1,0:T(8,128)(2,1)S(1)} %constant_dynamic-slice_fusion.2.mesh_ref, bf16[512,256]{1,0:T(8,128)(2,1)} %get-tuple-element.25, bf16[512,256]{1,0:T(8,128)(2,1)} %get-tuple-element.26), kind=kOutput, calls=%fused_computation.4 | convolution fusion | flops 168984576 | bytes 1179648 | tf_op jit(solution)/shard_map/dot_general | solution.py:221
  61.2 0.0 copy-start.6
  61.2 0.6 fusion
  61.8 1.5 %copy.16 = bf16[40,4,8,512]{3,2,1,0:T(8,128)(2,1)} copy(bf16[40,4,8,512]{3,0,2,1:T(8,128)(2,1)S(1)} %fusion) | data formatting | bytes 2621440 | tf_op jit(solution)/shard_map/convert_element_type | solution.py:229
  63.3 1.0 broadcast_select_fusion.1
  64.3 0.8 pad_maximum_fusion.2.out_weight_ref
  65.1 0.8 pad_maximum_fusion.1.value_ref
  66.0 0.0 collective-permute-done.1.low_other
  66.0 31.9 %attend.1 = bf16[320,512]{1,0:T(8,128)(2,1)} custom-call(s32[5120]{0:T(1024)} %reshape.108.order_ref, bf16[8192,512]{1,0:T(8,128)(2,1)} %grid_ref.1, bf16[1024,512]{1,0:T(8,128)(2,1)} %collective-permute-done.low_own, bf16[1024,512]{1,0:T(8,128)(2,1)} %collective-permute-done.1.low_other, bf16[1024,512]{1,0:T(8,128)(2,1)} %copy-done.2, ...), custom_call_target="tpu_custom_call" | custom-call | tf_op jit(solution)/shard_map/attend/pallas_call | solution.py:250
  97.9 0.9 constant_dynamic-slice_fusion
  98.8 0.5 collective-permute-start.10
  99.4 1.0 %collective-permute-done.10 = bf16[320,256]{1,0:T(8,128)(2,1)S(1)} collective-permute-done((bf16[320,256]{1,0:T(8,128)(2,1)S(1)}, bf16[320,256]{1,0:T(8,128)(2,1)S(1)}, u32[]{:S(2)}, u32[]{:S(2)}) %collective-permute-start.10) | collective-permute-done | bytes 163872 | tf_op jit(solution)/shard_map/ppermute | solution.py:165
  100.4 1.0 broadcast_select_fusion.9
  101.4 0.7 pad_maximum_fusion.3
  (24 shorter events, 0.1 us)
Async XLA Ops:
  0.0 2.4 %copy-start = (bf16[640,512]{1,0:T(8,128)(2,1)S(1)}, bf16[640,512]{1,0:T(8,128)(2,1)}, u32[]{:S(2)}) copy-start(bf16[640,512]{1,0:T(8,128)(2,1)} %param.10) | copy-start | bytes 1966084
  0.0 7.5 %collective-permute-start.9 = (bf16[256]{0:T(256)(128)(2,1)}, bf16[256]{0:T(256)(128)(2,1)S(1)}, u32[]{:S(2)}, u32[]{:S(2)}) collective-permute-start(bf16[256]{0:T(256)(128)(2,1)} %param.17), channel_id=1, source_target_pairs={{0,1},{1,0},{2,3},{3,2},{4,5},{5,4},{6,7},{7,6},{8,9},{9,8},{10,11... | collective-permute-start | bytes 1544 | tf_op jit(solution)/shard_map/ppermute | solution.py:165
  1.3 8.1 %collective-permute-start.6 = (bf16[320,32]{0,1:T(8,128)(2,1)S(1)}, bf16[320,32]{0,1:T(8,128)(2,1)S(1)}, u32[]{:S(2)}, u32[]{:S(2)}) collective-permute-start(bf16[320,32]{0,1:T(8,128)(2,1)S(1)} %constant_dynamic-slice_fusion.1), channel_id=1, source_target_pairs={{0,1},{1,0},{2,3},{3,2},{4,5},{5,4},{6,7},{7,6},{8,9},{9,8},{10,11... | collective-permute-start | bytes 61448 | tf_op jit(solution)/shard_map/ppermute | solution.py:165
  1.4 16.8 %collective-permute-start.5 = (bf16[512,256]{1,0:T(8,128)(2,1)}, bf16[512,256]{1,0:T(8,128)(2,1)S(1)}, u32[]{:S(2)}, u32[]{:S(2)}) collective-permute-start(bf16[512,256]{1,0:T(8,128)(2,1)} %param.13), channel_id=1, source_target_pairs={{0,1},{1,0},{2,3},{3,2},{4,5},{5,4},{6,7},{7,6},{8,9},{9,8},{10,11... | collective-permute-start | bytes 786440 | tf_op jit(solution)/shard_map/ppermute | solution.py:165
  1.8 15.2 %collective-permute-start.4 = (bf16[512,256]{1,0:T(8,128)(2,1)}, bf16[512,256]{1,0:T(8,128)(2,1)}, u32[]{:S(2)}, u32[]{:S(2)}) collective-permute-start(bf16[512,256]{1,0:T(8,128)(2,1)} %param.14), channel_id=1, source_target_pairs={{0,1},{1,0},{2,3},{3,2},{4,5},{5,4},{6,7},{7,6},{8,9},{9,8},{10,11... | collective-permute-start | bytes 786440 | tf_op jit(solution)/shard_map/ppermute | solution.py:165
  1.9 16.3 %collective-permute-start.7 = (bf16[512,256]{1,0:T(8,128)(2,1)}, bf16[512,256]{1,0:T(8,128)(2,1)S(1)}, u32[]{:S(2)}, u32[]{:S(2)}) collective-permute-start(bf16[512,256]{1,0:T(8,128)(2,1)} %param.15), channel_id=1, source_target_pairs={{0,1},{1,0},{2,3},{3,2},{4,5},{5,4},{6,7},{7,6},{8,9},{9,8},{10,11... | collective-permute-start | bytes 786440 | tf_op jit(solution)/shard_map/ppermute | solution.py:165
  2.4 57.5 %copy-start.1 = (bf16[320,512]{1,0:T(8,128)(2,1)}, bf16[320,512]{1,0:T(8,128)(2,1)S(1)}, u32[]{:S(2)}) copy-start(bf16[320,512]{1,0:T(8,128)(2,1)S(1)} %constant_dynamic-slice_fusion.2.mesh_ref) | copy-start | bytes 983044
  2.4 6.4 %copy-start.8 = (bf16[256]{0:T(256)(128)(2,1)S(1)}, bf16[256]{0:T(256)(128)(2,1)}, u32[]{:S(2)}) copy-start(bf16[256]{0:T(256)(128)(2,1)} %param.17) | copy-start | bytes 1540
  2.4 13.1 %copy-start.7 = (bf16[640,32]{0,1:T(8,128)(2,1)S(1)}, bf16[640,32]{0,1:T(8,128)(2,1)}, u32[]{:S(2)}) copy-start(bf16[640,32]{0,1:T(8,128)(2,1)} %param.12) | copy-start | bytes 122884
  6.7 11.6 %copy-start.4 = (bf16[512,256]{1,0:T(8,128)(2,1)S(1)}, bf16[512,256]{1,0:T(8,128)(2,1)}, u32[]{:S(2)}) copy-start(bf16[512,256]{1,0:T(8,128)(2,1)} %param.15) | copy-start | bytes 786436
  6.7 11.6 %copy-start.5 = (bf16[512,256]{1,0:T(8,128)(2,1)S(1)}, bf16[512,256]{1,0:T(8,128)(2,1)}, u32[]{:S(2)}) copy-start(bf16[512,256]{1,0:T(8,128)(2,1)} %param.13) | copy-start | bytes 786436
  7.5 28.7 %collective-permute-start.2 = (bf16[1024,512]{1,0:T(8,128)(2,1)}, bf16[1024,512]{1,0:T(8,128)(2,1)S(1)}, u32[]{:S(2)}, u32[]{:S(2)}) collective-permute-start(bf16[1024,512]{1,0:T(8,128)(2,1)} %get-tuple-element.7), channel_id=1, source_target_pairs={{2,0},{4,2},{6,4},{8,6},{10,8},{12,10},{14,12},{16,14},{18,16},{20... | collective-permute-start | bytes 3145736 | tf_op jit(solution)/shard_map/ppermute | solution.py:200
  9.4 50.2 %collective-permute-start = (bf16[1024,512]{1,0:T(8,128)(2,1)}, bf16[1024,512]{1,0:T(8,128)(2,1)}, u32[]{:S(2)}, u32[]{:S(2)}) collective-permute-start(bf16[1024,512]{1,0:T(8,128)(2,1)} %get-tuple-element.8), channel_id=1, source_target_pairs={{0,2},{2,4},{4,6},{6,8},{8,10},{10,12},{12,14},{14,16},{16,18},{18... | collective-permute-start | bytes 3145736 | tf_op jit(solution)/shard_map/ppermute | solution.py:197
  17.0 46.3 %collective-permute-start.8 = (bf16[256,512]{1,0:T(8,128)(2,1)}, bf16[256,512]{1,0:T(8,128)(2,1)}, u32[]{:S(2)}, u32[]{:S(2)}) collective-permute-start(bf16[256,512]{1,0:T(8,128)(2,1)} %param.16), channel_id=1, source_target_pairs={{0,1},{1,0},{2,3},{3,2},{4,5},{5,4},{6,7},{7,6},{8,9},{9,8},{10,11... | collective-permute-start | bytes 786440 | tf_op jit(solution)/shard_map/ppermute | solution.py:165
  36.2 25.6 %copy-start.2 = (bf16[1024,512]{1,0:T(8,128)(2,1)}, bf16[1024,512]{1,0:T(8,128)(2,1)S(1)}, u32[]{:S(2)}) copy-start(bf16[1024,512]{1,0:T(8,128)(2,1)S(1)} %collective-permute-done.2.high_own) | copy-start | bytes 3145732
  36.2 29.8 %collective-permute-start.3 = (bf16[1024,512]{1,0:T(8,128)(2,1)S(1)}, bf16[1024,512]{1,0:T(8,128)(2,1)}, u32[]{:S(2)}, u32[]{:S(2)}) collective-permute-start(bf16[1024,512]{1,0:T(8,128)(2,1)S(1)} %collective-permute-done.2.high_own), channel_id=1, source_target_pairs={{0,1},{1,0},{2,3},{3,2},{4,5},{5,4},{6,7},{7,6},{8,9},{9,8},{10,11... | collective-permute-start | bytes 3145736 | tf_op jit(solution)/shard_map/ppermute | solution.py:165
  59.6 6.4 %collective-permute-start.1 = (bf16[1024,512]{1,0:T(8,128)(2,1)}, bf16[1024,512]{1,0:T(8,128)(2,1)}, u32[]{:S(2)}, u32[]{:S(2)}) collective-permute-start(bf16[1024,512]{1,0:T(8,128)(2,1)} %collective-permute-done.low_own), channel_id=1, source_target_pairs={{0,1},{1,0},{2,3},{3,2},{4,5},{5,4},{6,7},{7,6},{8,9},{9,8},{10,11... | collective-permute-start | bytes 3145736 | tf_op jit(solution)/shard_map/ppermute | solution.py:165
  61.2 2.1 %copy-start.6 = (bf16[256,512]{1,0:T(8,128)(2,1)S(1)}, bf16[256,512]{1,0:T(8,128)(2,1)}, u32[]{:S(2)}) copy-start(bf16[256,512]{1,0:T(8,128)(2,1)} %param.16) | copy-start | bytes 786436
  61.8 3.3 %copy-start.3 = (bf16[512,256]{1,0:T(8,128)(2,1)S(1)}, bf16[512,256]{1,0:T(8,128)(2,1)}, u32[]{:S(2)}) copy-start(bf16[512,256]{1,0:T(8,128)(2,1)} %get-tuple-element.12) | copy-start | bytes 786436
  98.8 1.6 %collective-permute-start.10 = (bf16[320,256]{1,0:T(8,128)(2,1)S(1)}, bf16[320,256]{1,0:T(8,128)(2,1)S(1)}, u32[]{:S(2)}, u32[]{:S(2)}) collective-permute-start(bf16[320,256]{1,0:T(8,128)(2,1)S(1)} %constant_dynamic-slice_fusion), channel_id=1, source_target_pairs={{0,1},{1,0},{2,3},{3,2},{4,5},{5,4},{6,7},{7,6},{8,9},{9,8},{10,11... | collective-permute-start | bytes 491528 | tf_op jit(solution)/shard_map/ppermute | solution.py:165
